TPU v7x, 32 devices: a whole 2x2x4 slice. The times are simulated.
32 devices in a mesh: seq: 8 (over y, x, core), head: 4 (over z).
Axes of the slice: x: 2, y: 2, z: 4, core: 2. Of those that a mesh axis runs over, the one named last changes fastest.
Arguments:
- latent: bfloat16 [1024, 1024], P('seq'), may hold values from -15 to 15
- probe: bfloat16 [1024, 1024], P('seq'), may hold values from -6 to 6
- time_embed: float32 [1024], replicated, may hold values from -6 to 6
- gain_attn: float32 [1024], replicated, may hold values from 0.1 to 1.9
- w_query: bfloat16 [1024, 1024], P(None, 'head'), may hold values from -0.625 to 0.625
- w_key: bfloat16 [1024, 1024], P(None, 'head'), may hold values from -11 to 11
- w_value: bfloat16 [1024, 1024], P(None, 'head'), may hold values from -0.1875 to 0.1875
- w_out: bfloat16 [1024, 1024], P('head'), may hold values from -0.1875 to 0.1875
- gain_mlp: float32 [1024], replicated, may hold values from 0.1 to 1.9
- w_in: bfloat16 [1024, 4096], P(None, 'head'), may hold values from -0.1875 to 0.1875
- w_down: bfloat16 [4096, 1024], P('head'), may hold values from -0.09375 to 0.09375
Outputs:
- latent_end: float32 [1024, 1024], P('seq')
- frame_trace: float32 [1024], P('seq')
- frame_logp: float32 [1024], P('seq')
- mean_logp: float32 [], replicated
All inputs are finite; a program needn't handle non-finite values.
Results may differ from a plain program's by a relative error of at most 0.03.
The roundings to bfloat16 on the way count: a program that leaves them out, or rounds other values in their place, can miss the bound.
Values may be sent and summed in bfloat16 or wider, within the bound.
A program may use at most 64 MiB of HBM per device.

v0:
```python
import math
import jax
import jax.numpy as jnp
from jax import lax
from jax.sharding import PartitionSpec as P

HEAD_DIM = 64
STEPS = 2
EPSILON = 1e-05
GELU_COEF = 0.044715
ROOT_TWO_PI = math.sqrt(2.0 / math.pi)


def norm_pair(values, tangent, norm_gain):
    meansq = jnp.mean(values * values, axis=-1, keepdims=True) + EPSILON
    inverse = lax.rsqrt(meansq)
    inner_mean = jnp.mean(values * tangent, axis=-1, keepdims=True)
    primal = values * inverse * norm_gain
    derived = (tangent * inverse - values * inverse**3 * inner_mean) * norm_gain
    return (primal.astype(jnp.bfloat16), derived.astype(jnp.bfloat16))


def gelu_pair(pre_act, tangent):
    cubic_arg = pre_act + GELU_COEF * pre_act**3
    tanh_value = jnp.tanh(ROOT_TWO_PI * cubic_arg)
    output = 0.5 * pre_act * (1.0 + tanh_value)
    slope_value = 0.5 * (1.0 + tanh_value) + 0.5 * pre_act * (
        1.0 - tanh_value * tanh_value
    ) * ROOT_TWO_PI * (1.0 + 3.0 * GELU_COEF * pre_act * pre_act)
    return (output.astype(jnp.bfloat16), (slope_value * tangent).astype(jnp.bfloat16))


def split_heads(matrix):
    return matrix.reshape(matrix.shape[0], -1, HEAD_DIM)


def score_pair(queries, query_tang, keys, key_tang):
    scale = HEAD_DIM ** (-0.5)
    scores = jnp.einsum("rhd,shd->hrs", queries, keys, preferred_element_type=jnp.float32) * scale
    score_tang = (
        jnp.einsum("rhd,shd->hrs", query_tang, keys, preferred_element_type=jnp.float32)
        + jnp.einsum("rhd,shd->hrs", queries, key_tang, preferred_element_type=jnp.float32)
    ) * scale
    return (scores, score_tang)


def attention(queries, query_tang, keys, vals, key_tang, val_tang):
    rows = queries.shape[0]
    local_cols = queries.shape[1]
    head_count = local_cols // HEAD_DIM
    query_heads = split_heads(queries)
    query_tang_heads = split_heads(query_tang)
    top_start = jnp.full((head_count, rows), -1e30, jnp.float32)
    piece = (
        lax.all_gather(keys, "seq", axis=0, tiled=True),
        lax.all_gather(vals, "seq", axis=0, tiled=True),
    )
    keys_piece = split_heads(piece[0])
    vals_piece = split_heads(piece[1])
    scale = HEAD_DIM ** (-0.5)
    scores = (
        jnp.einsum("rhd,shd->hrs", query_heads, keys_piece, preferred_element_type=jnp.float32)
        * scale
    )
    new_top = jnp.maximum(top_start, jnp.max(scores, axis=-1))
    weights = jnp.exp(scores - new_top[:, :, None])
    total = jnp.sum(weights, axis=-1)
    add_primal = jnp.einsum(
        "hrs,shd->rhd", weights.astype(jnp.bfloat16), vals_piece, preferred_element_type=jnp.float32
    )
    row_top, total, acc_primal = (new_top, total, add_primal)
    piece = (
        lax.all_gather(keys, "seq", axis=0, tiled=True),
        lax.all_gather(vals, "seq", axis=0, tiled=True),
        lax.all_gather(key_tang, "seq", axis=0, tiled=True),
        lax.all_gather(val_tang, "seq", axis=0, tiled=True),
    )
    keys_piece = split_heads(piece[0])
    vals_piece = split_heads(piece[1])
    key_tang_piece = split_heads(piece[2])
    val_tang_piece = split_heads(piece[3])
    scores, score_tang = score_pair(query_heads, query_tang_heads, keys_piece, key_tang_piece)
    weights = jnp.exp(scores - row_top[:, :, None])
    weighted = weights * score_tang
    rounded = weights.astype(jnp.bfloat16)
    rounded_tang = weighted.astype(jnp.bfloat16)
    add_tang = jnp.einsum(
        "hrs,shd->rhd", rounded_tang, vals_piece, preferred_element_type=jnp.float32
    ) + jnp.einsum("hrs,shd->rhd", rounded, val_tang_piece, preferred_element_type=jnp.float32)
    carried = jnp.sum(weighted, axis=-1)
    total_t = jnp.transpose(total)[:, :, None]
    carried_t = jnp.transpose(carried)[:, :, None]
    primal = acc_primal / total_t
    tangent = add_tang / total_t - carried_t / total_t * primal
    return (
        primal.reshape(rows, local_cols).astype(jnp.bfloat16),
        tangent.reshape(rows, local_cols).astype(jnp.bfloat16),
    )


def attend_rows(normed, normed_tang, w_query, w_key, w_value):
    rows = normed.shape[0]
    stacked = jnp.concatenate([normed, normed_tang], axis=0)

    def project(weight):
        both = jnp.dot(stacked, weight, preferred_element_type=jnp.float32).astype(jnp.bfloat16)
        return (both[:rows], both[rows:])

    queries, query_tang = project(w_query)
    keys, key_tang = project(w_key)
    vals, val_tang = project(w_value)
    return attention(queries, query_tang, keys, vals, key_tang, val_tang)


def hidden_pair(normed_mlp, normed_mlp_tang, w_in):
    rows = normed_mlp.shape[0]
    pre_both = jnp.dot(
        jnp.concatenate([normed_mlp, normed_mlp_tang], axis=0),
        w_in,
        preferred_element_type=jnp.float32,
    )
    return gelu_pair(pre_both[:rows], pre_both[rows:])


def whole_field(
    inputs, direction, gain_attn, w_query, w_key, w_value, w_out, gain_mlp, w_in, w_down
):
    rows = inputs.shape[0]
    normed, normed_tang = norm_pair(inputs, direction, gain_attn)
    head_out, head_tang = attend_rows(normed, normed_tang, w_query, w_key, w_value)
    attn_terms = jnp.dot(
        jnp.concatenate([head_out, head_tang], axis=0), w_out, preferred_element_type=jnp.float32
    )
    attn_both = lax.psum(attn_terms, "head")
    attn = attn_both[:rows]
    attn_tang = attn_both[rows:]
    middle = inputs + attn
    middle_tang = direction + attn_tang
    normed_mlp, normed_mlp_tang = norm_pair(middle, middle_tang, gain_mlp)
    activ, activ_tang = hidden_pair(normed_mlp, normed_mlp_tang, w_in)
    mlp_terms = jnp.dot(
        jnp.concatenate([activ, activ_tang], axis=0), w_down, preferred_element_type=jnp.float32
    )
    mlp_both = lax.psum(mlp_terms, "head")
    return (attn + mlp_both[:rows], attn_tang + mlp_both[rows:])


def per_device(
    latent, probe, time_embed, gain_attn, w_query, w_key, w_value, w_out, gain_mlp, w_in, w_down
):
    rows = latent.shape[0]
    width = latent.shape[1]
    state = latent.astype(jnp.float32)
    direction = probe.astype(jnp.float32)
    trace = jnp.zeros((rows,), jnp.float32)
    for euler_step in range(STEPS):
        inputs = state + euler_step / STEPS * time_embed
        field, field_tang = whole_field(
            inputs, direction, gain_attn, w_query, w_key, w_value, w_out, gain_mlp, w_in, w_down
        )
        trace = trace + jnp.sum(direction * field_tang, axis=-1) / (STEPS * width)
        state = state + field / STEPS
    frame_logp = (
        trace - 0.5 * jnp.sum(state * state, axis=-1) / width - 0.5 * math.log(2.0 * math.pi)
    )
    grand_total = lax.psum(jnp.sum(frame_logp), "seq")
    mean_logp = grand_total / (rows * lax.axis_size("seq"))
    return (state, trace, frame_logp, mean_logp)


def solution(mesh):
    return jax.shard_map(
        per_device,
        mesh=mesh,
        in_specs=(
            P("seq", None),
            P("seq", None),
            P(),
            P(),
            P(None, "head"),
            P(None, "head"),
            P(None, "head"),
            P("head", None),
            P(),
            P(None, "head"),
            P("head", None),
        ),
        out_specs=(P("seq", None), P("seq"), P("seq"), P()),
        check_vma=False,
    )
```

profile of v0, /device:TPU:0, one launch (start us, length us, event | category | flops | bytes accessed | tf_op | source)
XLA Modules:
  0.0 390.4 jit_solution(14046082699471560486)
XLA Ops:
  8.1 1.2 fusion.22
  9.3 1.3 fusion.24
  10.7 1.5 convolution_convert_fusion.3
  12.2 11.3 %all_gather.29 = bf16[1024,256]{1,0:T(8,128)(2,1)S(1)} all-gather(bf16[128,256]{1,0:T(8,128)(2,1)S(1)} %get-tuple-element.42), channel_id=1, replica_groups=mesh['seq'=8,'head'=4] {'seq'}, dimensions={0}, use_global_device_ids=true | all-gather | bytes 589824 | tf_op jit(solution)/shard_map/all_gather | solution.py:55
  23.8 1.5 convolution_convert_fusion.4
  25.3 1.8 multiply_reduce_fusion.1
  27.1 1.8 fusion.113
  28.9 9.8 %all_gather.30 = bf16[1024,256]{1,0:T(8,128)(2,1)S(1)} all-gather(bf16[128,256]{1,0:T(8,128)(2,1)S(1)} %get-tuple-element.41), channel_id=1, replica_groups=mesh['seq'=8,'head'=4] {'seq'}, dimensions={0}, use_global_device_ids=true | all-gather | bytes 589824 | tf_op jit(solution)/shard_map/all_gather | solution.py:75
  38.9 1.5 convolution_convert_fusion.5
  40.4 9.9 %all_gather.28 = bf16[1024,256]{1,0:T(8,128)(2,1)} all-gather(bf16[128,256]{1,0:T(8,128)(2,1)S(1)} %get-tuple-element.40), channel_id=1, replica_groups=mesh['seq'=8,'head'=4] {'seq'}, dimensions={0}, use_global_device_ids=true | all-gather | bytes 589824 | tf_op jit(solution)/shard_map/all_gather | solution.py:56
  50.4 1.2 copy.27
  51.6 2.2 fusion
  53.9 2.5 fusion.109
  58.1 10.7 %all_gather.31 = bf16[1024,256]{1,0:T(8,128)(2,1)} all-gather(bf16[128,256]{1,0:T(8,128)(2,1)S(1)} %get-tuple-element.39), channel_id=1, replica_groups=mesh['seq'=8,'head'=4] {'seq'}, dimensions={0}, use_global_device_ids=true | all-gather | bytes 589824 | tf_op jit(solution)/shard_map/all_gather | solution.py:76
  68.8 1.3 copy.30
  70.1 2.2 fusion.12
  72.4 1.4 fusion.77
  73.8 52.3 %all-reduce.5.cloned.1.call-done = f32[256,1024]{1,0:T(8,128)} async-done(((f32[256,1024]{1,0:T(8,128)}), f32[256,1024]{1,0:T(8,128)}) %all-reduce.5.cloned.1.call-update) | async-done | bytes 1048592 | tf_op jit(solution)/shard_map/psum | solution.py:134
  126.1 1.6 multiply_reduce_fusion.7
  127.7 1.2 multiply_convert_fusion.6
  130.5 1.7 fusion.61
  132.3 51.3 %all-reduce.7.cloned.1.call-done = f32[256,1024]{1,0:T(8,128)} async-done(((f32[256,1024]{1,0:T(8,128)}), f32[256,1024]{1,0:T(8,128)}) %all-reduce.7.cloned.1.call-update) | async-done | bytes 1048592 | tf_op jit(solution)/shard_map/psum | solution.py:144
  183.6 1.4 multiply_reduce_fusion.5
  185.7 1.0 convolution_convert_fusion.1
  187.7 11.0 %all_gather.33 = bf16[1024,256]{1,0:T(8,128)(2,1)} all-gather(bf16[128,256]{1,0:T(8,128)(2,1)S(1)} %get-tuple-element.36), channel_id=1, replica_groups=mesh['seq'=8,'head'=4] {'seq'}, dimensions={0}, use_global_device_ids=true | all-gather | bytes 589824 | tf_op jit(solution)/shard_map/all_gather | solution.py:55
  198.7 2.0 copy.32
  201.7 2.9 multiply_reduce_fusion
  204.6 1.8 fusion.114
  206.3 10.7 %all_gather.34 = bf16[1024,256]{1,0:T(8,128)(2,1)} all-gather(bf16[128,256]{1,0:T(8,128)(2,1)S(1)} %get-tuple-element.35), channel_id=1, replica_groups=mesh['seq'=8,'head'=4] {'seq'}, dimensions={0}, use_global_device_ids=true | all-gather | bytes 589824 | tf_op jit(solution)/shard_map/all_gather | solution.py:75
  217.0 2.1 copy.33
  219.1 1.5 fusion.103
  220.6 9.9 %all_gather.32 = bf16[1024,256]{1,0:T(8,128)(2,1)} all-gather(bf16[128,256]{1,0:T(8,128)(2,1)S(1)} %get-tuple-element.34), channel_id=1, replica_groups=mesh['seq'=8,'head'=4] {'seq'}, dimensions={0}, use_global_device_ids=true | all-gather | bytes 589824 | tf_op jit(solution)/shard_map/all_gather | solution.py:56
  230.5 2.1 copy.31
  232.6 2.2 fusion.2
  234.8 2.7 fusion.111
  238.2 1.2 fusion.112
  239.4 1.1 fusion.14
  240.5 10.7 %all_gather.35 = bf16[1024,256]{1,0:T(8,128)(2,1)} all-gather(bf16[128,256]{1,0:T(8,128)(2,1)S(1)} %copy-done.16), channel_id=1, replica_groups=mesh['seq'=8,'head'=4] {'seq'}, dimensions={0}, use_global_device_ids=true | all-gather | bytes 589824 | tf_op jit(solution)/shard_map/all_gather | solution.py:76
  251.2 2.0 copy.34
  253.2 2.4 fusion.13
  255.6 1.4 fusion.81
  257.1 50.3 %all-reduce.9.cloned.1.call-done = f32[256,1024]{1,0:T(8,128)} async-done(((f32[256,1024]{1,0:T(8,128)}), f32[256,1024]{1,0:T(8,128)}) %all-reduce.9.cloned.1.call-update) | async-done | bytes 1048592 | tf_op jit(solution)/shard_map/psum | solution.py:134
  307.4 1.9 multiply_reduce_fusion.4
  311.2 1.7 fusion.69
  312.9 51.3 %all-reduce.11.cloned.1.call-done = f32[256,1024]{1,0:T(8,128)} async-done(((f32[256,1024]{1,0:T(8,128)}), f32[256,1024]{1,0:T(8,128)}) %all-reduce.11.cloned.1.call-update) | async-done | bytes 1048592 | tf_op jit(solution)/shard_map/psum | solution.py:144
  364.2 2.5 multiply_reduce_fusion.2
  366.7 1.1 fusion.101
  367.8 14.3 %psum.39 = f32[]{:T(128)} all-reduce(f32[]{:T(128)} %get-tuple-element.13), channel_id=1, replica_groups=mesh['seq'=8,'head'=4] {'seq'}, use_global_device_ids=true, to_apply=%region_22.0 | all-reduce | flops 1 | bytes 8 | tf_op jit(solution)/shard_map/psum | solution.py:166
  (83 shorter events, 9.8 us)
Async XLA Ops:
  7.2 121.8 %copy-start = (bf16[1024,1024]{1,0:T(8,128)(2,1)S(1)}, bf16[1024,1024]{1,0:T(8,128)(2,1)}, u32[]{:S(2)}) copy-start(bf16[1024,1024]{1,0:T(8,128)(2,1)} %param.20) | copy-start | bytes 6291460
  7.2 118.9 %all-reduce.5.cloned.1.call-start = ((), (), s32[]{:S(2)}) async-start(), calls=%async_computation | async-start | bytes 2097152 | tf_op jit(solution)/shard_map/psum | solution.py:134
  10.6 1.6 copy-start.15
  10.7 13.1 %copy-start.14 = (bf16[128,1024]{1,0:T(8,128)(2,1)}, bf16[128,1024]{1,0:T(8,128)(2,1)S(1)}, u32[]{:S(2)}) copy-start(bf16[128,1024]{1,0:T(8,128)(2,1)S(1)} %get-tuple-element.31) | copy-start | bytes 786436
  51.6 2.2 copy-start.1
  68.8 3.5 copy-start.12
  72.3 53.7 %copy-start.3 = (bf16[128,1024]{1,0:T(8,128)(2,1)S(1)}, bf16[128,1024]{1,0:T(8,128)(2,1)}, u32[]{:S(2)}) copy-start(bf16[128,1024]{1,0:T(8,128)(2,1)} %param.12) | copy-start | bytes 786436
  72.4 55.3 %copy-start.19 = (f32[1024]{0:T(1024)S(1)}, f32[1024]{0:T(1024)}, u32[]{:S(2)}) copy-start(f32[1024]{0:T(1024)} %param.19) | copy-start | bytes 12292
  73.7 109.8 %all-reduce.7.cloned.1.call-start = ((), (), s32[]{:S(2)}) async-start(), calls=%async_computation.1 | async-start | bytes 2097152 | tf_op jit(solution)/shard_map/psum | solution.py:144
  126.1 1.6 copy-start.4
  128.9 1.6 copy-start.5
  132.2 52.8 %copy-start.18 = (f32[1024]{0:T(1024)S(1)}, f32[1024]{0:T(1024)}, u32[]{:S(2)}) copy-start(f32[1024]{0:T(1024)} %param.14) | copy-start | bytes 12292
  132.3 175.1 %all-reduce.9.cloned.1.call-start = ((), (), s32[]{:S(2)}) async-start(), calls=%async_computation.2 | async-start | bytes 2097152 | tf_op jit(solution)/shard_map/psum | solution.py:134
  183.6 1.8 copy-start.20
  183.6 2.1 copy-start.21
  185.0 1.7 copy-start.7
  185.1 1.6 copy-start.22
  200.7 3.8 copy-start.11
  232.6 2.2 copy-start.2
  234.8 3.4 copy-start.10
  238.2 2.3 copy-start.16
  253.2 2.4 copy-start.13
  253.2 2.4 copy-start.17
  257.0 107.2 %all-reduce.11.cloned.1.call-start = ((), (), s32[]{:S(2)}) async-start(), calls=%async_computation.3 | async-start | bytes 2097152 | tf_op jit(solution)/shard_map/psum | solution.py:144
  307.4 1.9 copy-start.9
  309.6 1.6 copy-start.6
  311.2 53.0 %copy-start.8 = (f32[128,1024]{1,0:T(8,128)S(1)}, f32[128,1024]{1,0:T(8,128)}, u32[]{:S(2)}) copy-start(f32[128,1024]{1,0:T(8,128)} %copy-done.7) | copy-start | bytes 1572868
Sparse Core Ops, SparseCore 0:
  73.9 52.1 all-reduce.4
  132.4 51.1 all-reduce.6
  257.1 50.2 all-reduce.8
  313.0 51.1 all-reduce.10
where the time goes:
time: 391 us; the launch traced here: 390 us
  waiting for transfers between devices  205 us (52%)
  blocking collectives  98.5 us (25%)
  matrix products  35.8 us (9%)
  other arithmetic  20.1 us (5%)
  between operations  16 us (4%)
  local copies, waits for them, and re-layouts  14.7 us (4%)
    psum x2, waiting for transfers between devices, whole_field(): attn_both = lax.psum(attn_terms, 'head')  103 us
    psum x2, waiting for transfers between devices, whole_field(): mlp_both = lax.psum(mlp_terms, 'head')  103 us
    all_gather x2, blocking collectives, attention(): lax.all_gather(keys, 'seq', axis=0, tiled=True)  22.4 us
    all_gather x2, blocking collectives, attention(): lax.all_gather(val_tang, 'seq', axis=0, tiled=True)  21.4 us
    all_gather x2, blocking collectives, attention(): lax.all_gather(key_tang, 'seq', axis=0, tiled=True)  20.5 us
    all_gather x2, blocking collectives, attention(): lax.all_gather(vals, 'seq', axis=0, tiled=True)  19.9 us
    psum x1, blocking collectives, per_device(): grand_total = lax.psum(jnp.sum(frame_logp), 'seq')  14.3 us
  transfers between devices with their start and end apart: 4, of which 4 were waited for; matrix products, arithmetic and copies ran while one was open for 0% of the time, Pallas kernels for 0%

commit v1 on v0

--- a/solution.py
+++ b/solution.py
@@ -141,7 +141,9 @@
     mlp_terms = jnp.dot(
         jnp.concatenate([activ, activ_tang], axis=0), w_down, preferred_element_type=jnp.float32
     )
-    mlp_both = lax.psum(mlp_terms, "head")
+    mlp_both = mlp_terms
+    for hop in (1, 2):
+        mlp_both = mlp_both + lax.ppermute(mlp_both, "head", [(dev, dev ^ hop) for dev in range(4)])
     return (attn + mlp_both[:rows], attn_tang + mlp_both[rows:])
 
 

time: 391 us -> 430 us (1.100)
  waiting for transfers between devices: 205 us -> 241 us
  starting transfers between devices: 0.16 us -> 5.44 us
    ppermute x0 -> x4, waiting for transfers between devices: none -> 138 us  [whole_field(): lax.ppermute(mlp_both, 'head', [(dev, dev ^ hop) for dev in range(4)])]
    psum x2 -> x0, waiting for transfers between devices: 103 us -> none  [whole_field(): mlp_both = lax.psum(mlp_terms, 'head')]
    ppermute x0 -> x4, starting transfers between devices: none -> 5.18 us  [whole_field(): lax.ppermute(mlp_both, 'head', [(dev, dev ^ hop) for dev in range(4)])]
  transfers between devices with their start and end apart: 4 -> 6, of which waited for: 4 -> 6; matrix products, arithmetic and copies ran while one was open for 0% -> 0% of each run, Pallas kernels for 0% -> 0%
where the time goes in v1:
time: 430 us; the launch traced here: 429 us
  waiting for transfers between devices  241 us (56%)
  blocking collectives  98.7 us (23%)
  matrix products  33.8 us (8%)
  other arithmetic  18.1 us (4%)
  between operations  16.3 us (4%)
  local copies, waits for them, and re-layouts  15.6 us (4%)
  starting transfers between devices  5.44 us (1%)
    ppermute x4, waiting for transfers between devices, whole_field(): lax.ppermute(mlp_both, 'head', [(dev, dev ^ hop) for dev in range(4)])  138 us
    psum x2, waiting for transfers between devices, whole_field(): attn_both = lax.psum(attn_terms, 'head')  103 us
    all_gather x2, blocking collectives, attention(): lax.all_gather(keys, 'seq', axis=0, tiled=True)  22.2 us
    all_gather x2, blocking collectives, attention(): lax.all_gather(val_tang, 'seq', axis=0, tiled=True)  21.6 us
    all_gather x2, blocking collectives, attention(): lax.all_gather(key_tang, 'seq', axis=0, tiled=True)  20.5 us
    all_gather x2, blocking collectives, attention(): lax.all_gather(vals, 'seq', axis=0, tiled=True)  19.9 us
    psum x1, blocking collectives, per_device(): grand_total = lax.psum(jnp.sum(frame_logp), 'seq')  14.5 us
  transfers between devices with their start and end apart: 6, of which 6 were waited for; matrix products, arithmetic and copies ran while one was open for 0% of the time, Pallas kernels for 0%

profile of v1, /device:TPU:0, one launch (start us, length us, event | category | flops | bytes accessed | tf_op | source)
XLA Modules:
  0.0 429.3 jit_solution(13410805094121252881)
XLA Ops:
  8.1 1.2 fusion.22
  9.3 1.3 fusion.24
  10.7 1.5 convolution_convert_fusion.3
  12.2 11.3 %all_gather.29 = bf16[1024,256]{1,0:T(8,128)(2,1)S(1)} all-gather(bf16[128,256]{1,0:T(8,128)(2,1)S(1)} %get-tuple-element.42), channel_id=1, replica_groups=mesh['seq'=8,'head'=4] {'seq'}, dimensions={0}, use_global_device_ids=true | all-gather | bytes 589824 | tf_op jit(solution)/shard_map/all_gather | solution.py:55
  23.8 1.5 convolution_convert_fusion.4
  25.3 1.8 multiply_reduce_fusion.1
  27.1 1.8 fusion.113
  28.9 9.8 %all_gather.30 = bf16[1024,256]{1,0:T(8,128)(2,1)S(1)} all-gather(bf16[128,256]{1,0:T(8,128)(2,1)S(1)} %get-tuple-element.41), channel_id=1, replica_groups=mesh['seq'=8,'head'=4] {'seq'}, dimensions={0}, use_global_device_ids=true | all-gather | bytes 589824 | tf_op jit(solution)/shard_map/all_gather | solution.py:75
  38.9 1.5 convolution_convert_fusion.5
  40.4 9.9 %all_gather.28 = bf16[1024,256]{1,0:T(8,128)(2,1)} all-gather(bf16[128,256]{1,0:T(8,128)(2,1)S(1)} %get-tuple-element.40), channel_id=1, replica_groups=mesh['seq'=8,'head'=4] {'seq'}, dimensions={0}, use_global_device_ids=true | all-gather | bytes 589824 | tf_op jit(solution)/shard_map/all_gather | solution.py:56
  50.4 1.2 copy.27
  51.6 2.2 fusion
  53.9 2.5 fusion.109
  58.1 10.7 %all_gather.31 = bf16[1024,256]{1,0:T(8,128)(2,1)} all-gather(bf16[128,256]{1,0:T(8,128)(2,1)S(1)} %get-tuple-element.39), channel_id=1, replica_groups=mesh['seq'=8,'head'=4] {'seq'}, dimensions={0}, use_global_device_ids=true | all-gather | bytes 589824 | tf_op jit(solution)/shard_map/all_gather | solution.py:76
  68.8 1.3 copy.30
  70.1 2.2 fusion.12
  72.4 1.3 fusion.77
  74.0 52.1 %all-reduce.3.cloned.1.call-done = f32[256,1024]{1,0:T(8,128)} async-done(((f32[256,1024]{1,0:T(8,128)}), f32[256,1024]{1,0:T(8,128)}) %all-reduce.3.cloned.1.call-update) | async-done | bytes 1048592 | tf_op jit(solution)/shard_map/psum | solution.py:134
  126.1 1.6 multiply_reduce_fusion.7
  127.7 1.2 multiply_convert_fusion.6
  131.2 1.4 collective-permute-start
  132.6 23.7 %collective-permute-done = f32[256,1024]{1,0:T(8,128)S(1)} collective-permute-done((f32[256,1024]{1,0:T(8,128)S(1)}, f32[256,1024]{1,0:T(8,128)S(1)}, u32[]{:S(2)}, u32[]{:S(2)}) %collective-permute-start) | collective-permute-done | bytes 1048608 | tf_op jit(solution)/shard_map/ppermute | solution.py:146
  156.5 1.2 collective-permute-start.1
  157.7 45.4 %collective-permute-done.1 = f32[256,1024]{1,0:T(8,128)S(1)} collective-permute-done((f32[256,1024]{1,0:T(8,128)S(1)}, f32[256,1024]{1,0:T(8,128)S(1)}, u32[]{:S(2)}, u32[]{:S(2)}) %collective-permute-start.1) | collective-permute-done | bytes 1048608 | tf_op jit(solution)/shard_map/ppermute | solution.py:146
  207.0 10.9 %all_gather.33 = bf16[1024,256]{1,0:T(8,128)(2,1)} all-gather(bf16[128,256]{1,0:T(8,128)(2,1)S(1)} %get-tuple-element.36), channel_id=1, replica_groups=mesh['seq'=8,'head'=4] {'seq'}, dimensions={0}, use_global_device_ids=true | all-gather | bytes 589824 | tf_op jit(solution)/shard_map/all_gather | solution.py:55
  217.9 2.0 copy.32
  220.9 2.9 multiply_reduce_fusion
  223.8 1.8 fusion.114
  225.5 10.7 %all_gather.34 = bf16[1024,256]{1,0:T(8,128)(2,1)} all-gather(bf16[128,256]{1,0:T(8,128)(2,1)S(1)} %get-tuple-element.35), channel_id=1, replica_groups=mesh['seq'=8,'head'=4] {'seq'}, dimensions={0}, use_global_device_ids=true | all-gather | bytes 589824 | tf_op jit(solution)/shard_map/all_gather | solution.py:75
  236.3 2.1 copy.33
  238.3 1.5 fusion.103
  239.8 9.9 %all_gather.32 = bf16[1024,256]{1,0:T(8,128)(2,1)} all-gather(bf16[128,256]{1,0:T(8,128)(2,1)S(1)} %get-tuple-element.34), channel_id=1, replica_groups=mesh['seq'=8,'head'=4] {'seq'}, dimensions={0}, use_global_device_ids=true | all-gather | bytes 589824 | tf_op jit(solution)/shard_map/all_gather | solution.py:56
  249.8 2.0 copy.31
  251.8 2.2 fusion.2
  254.0 2.8 fusion.111
  257.4 1.2 fusion.112
  258.6 1.1 fusion.14
  259.7 10.9 %all_gather.35 = bf16[1024,256]{1,0:T(8,128)(2,1)} all-gather(bf16[128,256]{1,0:T(8,128)(2,1)S(1)} %copy-done.18), channel_id=1, replica_groups=mesh['seq'=8,'head'=4] {'seq'}, dimensions={0}, use_global_device_ids=true | all-gather | bytes 589824 | tf_op jit(solution)/shard_map/all_gather | solution.py:76
  270.6 2.0 copy.34
  272.7 2.4 fusion.13
  275.1 1.3 fusion.81
  276.4 51.1 %all-reduce.5.cloned.1.call-done = f32[256,1024]{1,0:T(8,128)} async-done(((f32[256,1024]{1,0:T(8,128)}), f32[256,1024]{1,0:T(8,128)}) %all-reduce.5.cloned.1.call-update) | async-done | bytes 1048592 | tf_op jit(solution)/shard_map/psum | solution.py:134
  327.6 1.9 multiply_reduce_fusion.4
  332.1 1.4 collective-permute-start.2
  333.5 23.7 %collective-permute-done.2 = f32[256,1024]{1,0:T(8,128)S(1)} collective-permute-done((f32[256,1024]{1,0:T(8,128)S(1)}, f32[256,1024]{1,0:T(8,128)S(1)}, u32[]{:S(2)}, u32[]{:S(2)}) %collective-permute-start.2) | collective-permute-done | bytes 1048608 | tf_op jit(solution)/shard_map/ppermute | solution.py:146
  357.3 1.2 collective-permute-start.3
  358.5 45.4 %collective-permute-done.3 = f32[256,1024]{1,0:T(8,128)S(1)} collective-permute-done((f32[256,1024]{1,0:T(8,128)S(1)}, f32[256,1024]{1,0:T(8,128)S(1)}, u32[]{:S(2)}, u32[]{:S(2)}) %collective-permute-start.3) | collective-permute-done | bytes 1048608 | tf_op jit(solution)/shard_map/ppermute | solution.py:146
  406.2 14.5 %psum.23 = f32[]{:T(128)} all-reduce(f32[]{:T(128)} %get-tuple-element.13), channel_id=1, replica_groups=mesh['seq'=8,'head'=4] {'seq'}, use_global_device_ids=true, to_apply=%region_20.0 | all-reduce | flops 1 | bytes 8 | tf_op jit(solution)/shard_map/psum | solution.py:168
  (93 shorter events, 16.2 us)
Async XLA Ops:
  7.2 121.8 %copy-start = (bf16[1024,1024]{1,0:T(8,128)(2,1)S(1)}, bf16[1024,1024]{1,0:T(8,128)(2,1)}, u32[]{:S(2)}) copy-start(bf16[1024,1024]{1,0:T(8,128)(2,1)} %param.20) | copy-start | bytes 6291460
  7.2 118.9 %all-reduce.3.cloned.1.call-start = ((), (), s32[]{:S(2)}) async-start(), calls=%async_computation | async-start | bytes 2097152 | tf_op jit(solution)/shard_map/psum | solution.py:134
  10.6 1.6 copy-start.17
  10.7 13.1 %copy-start.16 = (bf16[128,1024]{1,0:T(8,128)(2,1)}, bf16[128,1024]{1,0:T(8,128)(2,1)S(1)}, u32[]{:S(2)}) copy-start(bf16[128,1024]{1,0:T(8,128)(2,1)S(1)} %get-tuple-element.31) | copy-start | bytes 786436
  51.6 2.2 copy-start.1
  68.8 3.5 copy-start.14
  72.3 53.7 %copy-start.3 = (bf16[128,1024]{1,0:T(8,128)(2,1)S(1)}, bf16[128,1024]{1,0:T(8,128)(2,1)}, u32[]{:S(2)}) copy-start(bf16[128,1024]{1,0:T(8,128)(2,1)} %param.12) | copy-start | bytes 786436
  72.4 55.3 %copy-start.21 = (f32[1024]{0:T(1024)S(1)}, f32[1024]{0:T(1024)}, u32[]{:S(2)}) copy-start(f32[1024]{0:T(1024)} %param.19) | copy-start | bytes 12292
  73.7 253.8 %all-reduce.5.cloned.1.call-start = ((), (), s32[]{:S(2)}) async-start(), calls=%async_computation.1 | async-start | bytes 2097152 | tf_op jit(solution)/shard_map/psum | solution.py:134
  126.1 1.6 copy-start.4
  128.9 1.6 copy-start.5
  131.2 25.1 %collective-permute-start = (f32[256,1024]{1,0:T(8,128)S(1)}, f32[256,1024]{1,0:T(8,128)S(1)}, u32[]{:S(2)}, u32[]{:S(2)}) collective-permute-start(f32[256,1024]{1,0:T(8,128)S(1)} %fusion.61), channel_id=1, source_target_pairs={{0,1},{1,0},{2,3},{3,2},{4,5},{5,4},{6,7},{7,6},{8,9},{9,8},{10,11... | collective-permute-start | bytes 3145736 | tf_op jit(solution)/shard_map/ppermute | solution.py:146
  156.5 46.8 %copy-start.10 = (bf16[128,1024]{1,0:T(8,128)(2,1)S(1)}, bf16[128,1024]{1,0:T(8,128)(2,1)}, u32[]{:S(2)}) copy-start(bf16[128,1024]{1,0:T(8,128)(2,1)} %param.11) | copy-start | bytes 786436
  156.5 47.1 %copy-start.20 = (f32[1024]{0:T(1024)S(1)}, f32[1024]{0:T(1024)}, u32[]{:S(2)}) copy-start(f32[1024]{0:T(1024)} %param.14) | copy-start | bytes 12292
  156.5 46.6 %collective-permute-start.1 = (f32[256,1024]{1,0:T(8,128)S(1)}, f32[256,1024]{1,0:T(8,128)S(1)}, u32[]{:S(2)}, u32[]{:S(2)}) collective-permute-start(f32[256,1024]{1,0:T(8,128)S(1)} %add.170), channel_id=1, source_target_pairs={{0,2},{1,3},{2,0},{3,1},{4,6},{5,7},{6,4},{7,5},{8,10},{9,11},{10,... | collective-permute-start | bytes 3145736 | tf_op jit(solution)/shard_map/ppermute | solution.py:146
  203.2 1.7 copy-start.13
  203.3 1.4 copy-start.22
  203.3 1.7 copy-start.23
  203.5 2.5 copy-start.7
  203.6 2.4 copy-start.24
  220.0 3.8 copy-start.12
  251.8 2.2 copy-start.2
  254.0 3.4 copy-start.11
  257.4 2.3 copy-start.18
  272.7 2.4 copy-start.15
  272.7 2.4 copy-start.19
  327.6 1.9 copy-start.9
  329.8 1.6 copy-start.6
  332.1 25.1 %collective-permute-start.2 = (f32[256,1024]{1,0:T(8,128)S(1)}, f32[256,1024]{1,0:T(8,128)S(1)}, u32[]{:S(2)}, u32[]{:S(2)}) collective-permute-start(f32[256,1024]{1,0:T(8,128)S(1)} %fusion.69), channel_id=1, source_target_pairs={{0,1},{1,0},{2,3},{3,2},{4,5},{5,4},{6,7},{7,6},{8,9},{9,8},{10,11... | collective-permute-start | bytes 3145736 | tf_op jit(solution)/shard_map/ppermute | solution.py:146
  357.3 46.7 %copy-start.8 = (f32[128,1024]{1,0:T(8,128)S(1)}, f32[128,1024]{1,0:T(8,128)}, u32[]{:S(2)}) copy-start(f32[128,1024]{1,0:T(8,128)} %copy-done.7) | copy-start | bytes 1572868
  357.3 46.6 %collective-permute-start.3 = (f32[256,1024]{1,0:T(8,128)S(1)}, f32[256,1024]{1,0:T(8,128)S(1)}, u32[]{:S(2)}, u32[]{:S(2)}) collective-permute-start(f32[256,1024]{1,0:T(8,128)S(1)} %add.187), channel_id=1, source_target_pairs={{0,2},{1,3},{2,0},{3,1},{4,6},{5,7},{6,4},{7,5},{8,10},{9,11},{10,... | collective-permute-start | bytes 3145736 | tf_op jit(solution)/shard_map/ppermute | solution.py:146
Sparse Core Ops, SparseCore 0:
  73.9 52.1 all-reduce.2
  276.6 50.9 all-reduce.4
